TPU v7x, 32 devices: a whole 2x2x4 slice. The times are simulated.
32 devices in a mesh: section: 4 (over z), expert: 4 (over y, x), dp: 2 (over core).
Axes of the slice: x: 2, y: 2, z: 4, core: 2. Of those that a mesh axis runs over, the one named last changes fastest.
Arguments:
- stash: bfloat16 [4, 256, 2048], P('section', 'dp', 'expert'), may hold values from -6 to 6
- cotangent: bfloat16 [4, 256, 2048], P('section', 'dp', 'expert'), may hold values from -6 to 6
- backward_expert_routes: int32 [4, 256, 2], P('section', 'dp'), may hold values from 0 to 3, all different within a row; in each aligned block of 128 rows (0 to 127, 128 to 255, ..., all dimensions but the last counted through in order) at most 80 rows name the same one
- backward_job_lengths: int32 [4, 4], P('section'), may hold values from 1 to 128, 256 in all within a row
- layer_norm_gains: float32 [4, 2048], P('section'), may hold values from 0.25 to 1.75
- router: bfloat16 [4, 2048, 4], P('section'), may hold values from -0.125 to 0.125
- expert_gate_weight: bfloat16 [4, 2048, 28672], P('section', None, ('expert', 'dp')), may hold values from -0.125 to 0.125
- expert_up_weight: bfloat16 [4, 2048, 28672], P('section', None, ('expert', 'dp')), may hold values from -0.125 to 0.125
- expert_down_weight: bfloat16 [4, 28672, 2048], P('section', ('expert', 'dp')), may hold values from -0.0625 to 0.0625
- adapter_down_maps: bfloat16 [4, 2048, 64], P('section', 'expert'), may hold values from -0.125 to 0.125
- adapter_up_maps: bfloat16 [4, 64, 2048], P('section', None, 'expert'), may hold values from -1.5 to 1.5
Outputs:
- handed_back: bfloat16 [4, 256, 2048], P('section', 'dp', 'expert')
- grad_lora_down: float32 [4, 2048, 64], P('section', 'expert')
- grad_lora_up: float32 [4, 64, 2048], P('section', None, 'expert')
Inputs may be any that keep to these rules, and one draw needn't show every extreme that they name: `backward_expert_routes`: each row names two different experts. In each aligned block of 128 rows (the tokens of one device) no expert is named more than 80 times. `backward_job_lengths`: each row sums to 256.
All inputs are finite; a program needn't handle non-finite values.
Results may differ from a plain program's by a relative error of at most 0.008.
Values may be sent and summed in bfloat16 or wider, within the bound.
A program may use at most 128 MiB of HBM per device.

v0:
```python
import jax
import jax.numpy as jnp
from jax import lax
from jax.sharding import PartitionSpec as P

MODEL_WIDTH = 2048
EXPERTS = 4
ADAPTER_RANK = 16
CAP = 80


EPS = 1e-05
ADAPTER_SCALE = 0.5
HIGH = lax.Precision.HIGHEST


def from_behind(block, axis, distance):
    devices = range(lax.axis_size(axis))
    route = [((i - distance) % len(devices), i) for i in devices]
    return lax.ppermute(block, axis, route)


def job_columns(job_token_lengths, offset, count):
    ends = jnp.cumsum(job_token_lengths, dtype=jnp.int32)
    position = offset + jnp.arange(count, dtype=jnp.int32)
    owner = jnp.sum((ends[None, :] <= position[:, None]).astype(jnp.int32), axis=1, dtype=jnp.int32)
    column_owner = (
        jnp.arange(job_token_lengths.shape[0] * ADAPTER_RANK, dtype=jnp.int32) // ADAPTER_RANK
    )
    return (owner[:, None] == column_owner[None, :]).astype(jnp.float32)


def prepare(whole_batch, norm_gain_vector, router, token_routes):
    expert_values = whole_batch.astype(jnp.float32)
    scale = lax.rsqrt(jnp.mean(expert_values * expert_values, axis=1, keepdims=True) + EPS)
    normalized_input = (expert_values * scale * norm_gain_vector[None, :]).astype(jnp.bfloat16)
    logits = jnp.dot(normalized_input, router, preferred_element_type=jnp.float32)
    labels = jnp.arange(router.shape[1], dtype=jnp.int32)
    first = (token_routes[:, 0:1] == labels[None, :]).astype(jnp.float32)
    second = (token_routes[:, 1:2] == labels[None, :]).astype(jnp.float32)
    upper = jax.nn.sigmoid(jnp.sum(first * logits, axis=1) - jnp.sum(second * logits, axis=1))
    table = upper[:, None] * first + (1.0 - upper)[:, None] * second
    return (expert_values, scale, normalized_input, first, second, upper, table)


def router_grad(gate_grad, first, second, upper):
    spread = jnp.sum(first * gate_grad, axis=1) - jnp.sum(second * gate_grad, axis=1)
    delta = spread * upper * (1.0 - upper)
    return delta[:, None] * (first - second)


def slot_matrix(member, capacity):
    marks = member.astype(jnp.int32)
    ranked = jnp.cumsum(marks, axis=-1, dtype=jnp.int32) - marks
    slots = jnp.arange(capacity, dtype=jnp.int32)
    hit = (ranked[..., None, :] == slots[:, None]) & (marks[..., None, :] == 1)
    return hit.astype(jnp.float32)


def expert_back(
    rows, adapter_gradient_list, expert_gate_weight, expert_up_weight, expert_down_weight
):
    gate = jnp.dot(rows, expert_gate_weight, preferred_element_type=jnp.float32)
    up = jnp.dot(rows, expert_up_weight, preferred_element_type=jnp.float32)
    sig = jax.nn.sigmoid(gate)
    act = gate * sig
    hidden = (act * up).astype(jnp.bfloat16)
    output = jnp.dot(hidden, expert_down_weight, preferred_element_type=jnp.float32)
    gate_term = jnp.sum(adapter_gradient_list.astype(jnp.float32) * output, axis=1)
    back = jnp.dot(adapter_gradient_list, expert_down_weight.T, preferred_element_type=jnp.float32)
    d_gate = (back * up * sig * (1.0 + gate * (1.0 - sig))).astype(jnp.bfloat16)
    d_up = (back * act).astype(jnp.bfloat16)
    d_rows = jnp.dot(d_gate, expert_gate_weight.T, preferred_element_type=jnp.float32) + jnp.dot(
        d_up, expert_up_weight.T, preferred_element_type=jnp.float32
    )
    return (d_rows, gate_term)


def body(
    stash,
    cotangent,
    backward_expert_routes,
    backward_job_lengths,
    layer_norm_gains,
    router,
    expert_gate_weight,
    expert_up_weight,
    expert_down_weight,
    adapter_down_maps,
    adapter_up_maps,
):
    groups = lax.axis_size("expert")
    shards = lax.axis_size("dp")
    column_block = lax.axis_index("expert")
    token_block = lax.axis_index("dp")
    mine = column_block // (groups // EXPERTS)
    s_cols = stash[0]
    gradient_columns = cotangent[0]
    count, width = s_cols.shape
    s_full, g_full = (
        lax.all_gather(s_cols, "expert", axis=1, tiled=True),
        lax.all_gather(gradient_columns, "expert", axis=1, tiled=True),
    )
    norm_gain_vector = layer_norm_gains[0]
    route_w = router[0]
    wg = expert_gate_weight[0]
    wu = expert_up_weight[0]
    wd = expert_down_weight[0]
    down_map_rows = adapter_down_maps[0]
    backward_columns = adapter_up_maps[0]
    col_start = column_block * width
    gain_cols = lax.dynamic_slice_in_dim(norm_gain_vector, col_start, width, 0)
    route_cols = lax.dynamic_slice_in_dim(route_w, col_start, width, 0)
    offset = token_block * count
    backward_mask = job_columns(backward_job_lengths[0], offset, count)
    b_values, b_scale, b_normed, b_first, b_second, b_upper, b_table = prepare(
        s_full, norm_gain_vector, route_w, backward_expert_routes[0]
    )
    labels = jnp.arange(EXPERTS, dtype=jnp.int32)
    own = (labels == mine).astype(jnp.float32)
    b_member = jnp.sum((b_first + b_second) * own[None, :], axis=1)
    b_gate = jnp.sum(b_table * own[None, :], axis=1)
    b_slots = slot_matrix(b_member, CAP)
    b_normed_cols = lax.dynamic_slice_in_dim(b_normed, col_start, width, 1)
    a_full = lax.all_gather(down_map_rows, "expert", axis=0, tiled=True)
    b_low = jnp.dot(b_normed, a_full, preferred_element_type=jnp.float32)
    grad_low_rank = lax.psum(
        jnp.dot(gradient_columns, backward_columns.T, preferred_element_type=jnp.float32), "expert"
    )
    backward_low_rank = (b_low * backward_mask).astype(jnp.bfloat16)
    grad_low_rank_backward = (ADAPTER_SCALE * grad_low_rank * backward_mask).astype(jnp.bfloat16)
    up_map_gradient = ADAPTER_SCALE * jnp.dot(
        backward_low_rank.T, gradient_columns, preferred_element_type=jnp.float32
    )
    down_map_gradient = jnp.dot(
        b_normed_cols.T, grad_low_rank_backward, preferred_element_type=jnp.float32
    )
    down_map_gradient, up_map_gradient = lax.psum((down_map_gradient, up_map_gradient), "dp")
    normalized_grad_adapter = jnp.dot(
        grad_low_rank_backward, down_map_rows.T, preferred_element_type=jnp.float32
    )
    b_slots_low = b_slots.astype(jnp.bfloat16)
    b_sel = jnp.dot(b_slots_low, b_normed, preferred_element_type=jnp.float32).astype(jnp.bfloat16)
    g_sel = jnp.dot(b_slots_low, g_full, preferred_element_type=jnp.float32).astype(jnp.bfloat16)
    b_rows, g_rows = (
        lax.all_gather(b_sel, "dp", axis=0, tiled=True),
        lax.all_gather(g_sel, "dp", axis=0, tiled=True),
    )
    dn_slots, dgam_slots = expert_back(b_rows, g_rows, wg, wu, wd)
    b_member_all, b_gate_all = (
        lax.all_gather(b_member, "dp", axis=0, tiled=True),
        lax.all_gather(b_gate, "dp", axis=0, tiled=True),
    )
    b_all = slot_matrix(b_member_all.reshape(shards, count), CAP)
    b_terms = jnp.einsum(
        "pct,pcex->eptx", b_all, dn_slots.reshape(shards, CAP, groups, width), precision=HIGH
    )
    b_terms = b_terms * b_gate_all.reshape(shards, count)[None, :, :, None]
    normalized_grad_experts = lax.psum_scatter(
        b_terms.reshape(groups * shards * count, width),
        ("expert", "dp"),
        scatter_dimension=0,
        tiled=True,
    )
    dgam_own = lax.psum_scatter(dgam_slots, "dp", scatter_dimension=0, tiled=True)
    dgam_tokens = jnp.dot(dgam_own, b_slots, precision=HIGH)
    gate_part = dgam_tokens[:, None] * own[None, :]
    expert_base_output = normalized_grad_experts + normalized_grad_adapter
    b_values_cols = lax.dynamic_slice_in_dim(b_values, col_start, width, 1)
    route_cols_t = route_cols.astype(jnp.float32).T
    base_weighted = expert_base_output * gain_cols[None, :]
    stat_part = jnp.sum(base_weighted * b_values_cols, axis=1, keepdims=True)
    gate_grad, stat_part = lax.psum((gate_part, stat_part), "expert")
    d_logit = router_grad(gate_grad, b_first, b_second, b_upper)
    lifted = jnp.dot(
        b_values * norm_gain_vector[None, :], route_w.astype(jnp.float32), precision=HIGH
    )
    stat = stat_part + jnp.sum(d_logit * lifted, axis=1, keepdims=True)
    weighted = base_weighted + jnp.dot(d_logit, route_cols_t, precision=HIGH) * gain_cols[None, :]
    layer_result = (
        gradient_columns.astype(jnp.float32)
        + b_scale * weighted
        - b_values_cols * b_scale * b_scale * b_scale * stat / MODEL_WIDTH
    )
    handed_back = from_behind(layer_result.astype(jnp.bfloat16), "section", -1)
    return (handed_back[None], down_map_gradient[None], up_map_gradient[None])


def solution(mesh):
    return jax.shard_map(
        body,
        mesh=mesh,
        in_specs=(
            P("section", "dp", "expert"),
            P("section", "dp", "expert"),
            P("section", "dp", None),
            P("section", None),
            P("section", None),
            P("section", None, None),
            P("section", None, ("expert", "dp")),
            P("section", None, ("expert", "dp")),
            P("section", ("expert", "dp"), None),
            P("section", "expert", None),
            P("section", None, "expert"),
        ),
        out_specs=(
            P("section", "dp", "expert"),
            P("section", "expert", None),
            P("section", None, "expert"),
        ),
        check_vma=False,
    )
```

profile of v0, /device:TPU:0, one launch (start us, length us, event | category | flops | bytes accessed | tf_op | source)
XLA Modules:
  0.0 168.8 jit_solution(5793704472606777799)
XLA Ops:
  8.1 12.0 %all-gather = bf16[1,128,2048]{2,1,0:T(8,128)(2,1)S(1)} all-gather(bf16[1,128,512]{2,1,0:T(8,128)(2,1)} %param.11), channel_id=2, replica_groups=mesh['section'=4,'expert'=4,'dp'=2] {'expert'}, dimensions={2}, use_global_device_ids=true | all-gather | bytes 655360 | tf_op jit(solution)/shard_map/all_gather | solution.py:101
  20.1 0.2 fusion.33
  20.3 0.8 slice_bitcast_fusion.1
  21.0 0.9 fusion.35
  21.9 1.0 select_reduce_fusion.2
  22.9 0.1 multiply_reduce_fusion
  23.0 1.8 %all-gather.3 = f32[2,1,128]{2,1,0:T(1,128)S(1)} all-gather(f32[1,1,128]{2,1,0:T(1,128)S(1)} %bitcast.144), channel_id=1, replica_groups=mesh['section'=4,'expert'=4,'dp'=2] {'dp'}, dimensions={0}, use_global_device_ids=true | all-gather | bytes 1536 | tf_op jit(solution)/shard_map/all_gather | solution.py:151
  24.9 0.1 copy.25
  25.0 0.2 reduce-window.16
  25.1 0.1 reduce
  25.3 9.7 %all-gather.1 = bf16[1,128,2048]{2,1,0:T(8,128)(2,1)S(1)} all-gather(bf16[1,128,512]{2,1,0:T(8,128)(2,1)S(1)} %copy-done.2), channel_id=3, replica_groups=mesh['section'=4,'expert'=4,'dp'=2] {'expert'}, dimensions={2}, use_global_device_ids=true | all-gather | bytes 655360 | tf_op jit(solution)/shard_map/all_gather | solution.py:102
  34.9 0.2 convolution_convert_fusion
  35.2 0.2 convolution_convert_fusion.1
  35.4 2.3 %all_gather.23 = bf16[160,2048]{1,0:T(8,128)(2,1)S(1)} all-gather(bf16[80,2048]{1,0:T(8,128)(2,1)S(1)} %convolution_convert_fusion.1), channel_id=1, replica_groups=mesh['section'=4,'expert'=4,'dp'=2] {'dp'}, dimensions={0}, use_global_device_ids=true | all-gather | bytes 983040 | tf_op jit(solution)/shard_map/all_gather | solution.py:147
  37.7 2.3 %all_gather.24 = bf16[160,2048]{1,0:T(8,128)(2,1)S(1)} all-gather(bf16[80,2048]{1,0:T(8,128)(2,1)S(1)} %convolution_convert_fusion), channel_id=1, replica_groups=mesh['section'=4,'expert'=4,'dp'=2] {'dp'}, dimensions={0}, use_global_device_ids=true | all-gather | bytes 983040 | tf_op jit(solution)/shard_map/all_gather | solution.py:146
  40.0 9.3 %fusion.2 = f32[160,3584]{1,0:T(8,128)} fusion(bf16[160,2048]{1,0:T(8,128)(2,1)S(1)} %all_gather.24, bf16[1,2048,3584]{2,1,0:T(8,128)(2,1)} %param.17), kind=kOutput, calls=%fused_computation.2 | convolution fusion | flops 2348810240 | bytes 17629184 | tf_op jit(solution)/shard_map/dot_general | solution.py:63
  49.3 0.9 copy-done.1
  50.1 3.9 %fusion.6 = f32[160,3584]{1,0:T(8,128)} fusion(bf16[160,2048]{1,0:T(8,128)(2,1)S(1)} %all_gather.24, bf16[1,2048,3584]{2,1,0:T(8,128)(2,1)S(1)} %copy-done.1), kind=kOutput, calls=%fused_computation.6 | convolution fusion | flops 2348810240 | bytes 17629184 | tf_op jit(solution)/shard_map/dot_general | solution.py:64
  54.1 11.6 %fusion.10 = f32[160,3584]{1,0:T(8,128)} fusion(bf16[160,2048]{1,0:T(8,128)(2,1)S(1)} %all_gather.23, bf16[1,3584,2048]{2,1,0:T(8,128)(2,1)} %param.19), kind=kOutput, calls=%fused_computation.10 | convolution fusion | flops 2348810240 | bytes 17629184 | tf_op jit(solution)/shard_map/dot_general | solution.py:70
  65.7 12.1 %fusion = f32[160,2048]{1,0:T(8,128)S(1)} fusion(bf16[1,2048,3584]{2,1,0:T(8,128)(2,1)} %param.17, f32[160,3584]{1,0:T(8,128)} %fusion.2, f32[160,3584]{1,0:T(8,128)} %fusion.10, f32[160,3584]{1,0:T(8,128)} %fusion.6), kind=kOutput, calls=%fused_computation | convolution fusion | flops 2354544640 | bytes 22872064 | tf_op jit(solution)/shard_map/dot_general | solution.py:73
  77.8 12.7 %fusion.15 = f32[160,2048]{1,0:T(8,128)} fusion(f32[160,2048]{1,0:T(8,128)S(1)} %fusion, bf16[1,2048,3584]{2,1,0:T(8,128)(2,1)} %param.18, f32[160,3584]{1,0:T(8,128)} %fusion.10, f32[160,3584]{1,0:T(8,128)} %fusion.2), kind=kOutput, calls=%fused_computation.13 | convolution fusion | flops 2352578560 | bytes 21889024 | tf_op jit(solution)/shard_map/dot_general | solution.py:73
  90.5 2.2 %reshape.159 = f32[2,80,4,512]{3,2,1,0:T(4,128)S(1)} reshape(f32[160,2048]{1,0:T(8,128)} %fusion.15) | data formatting | bytes 2621440 | tf_op jit(solution)/shard_map/reshape | solution.py:156
  92.7 0.3 reduce_window_sum.25
  93.0 1.8 %all-gather.4 = f32[2,1,128]{2,1,0:T(1,128)S(1)} all-gather(f32[1,1,128]{2,1,0:T(1,128)S(1)} %bitcast.143), channel_id=1, replica_groups=mesh['section'=4,'expert'=4,'dp'=2] {'dp'}, dimensions={0}, use_global_device_ids=true | all-gather | bytes 1536 | tf_op jit(solution)/shard_map/all_gather | solution.py:152
  94.8 1.5 multiply_bitcast_fusion
  96.4 1.6 copy.28
  98.1 0.2 reduce-window.17
  98.3 0.2 fusion.48
  98.4 15.4 %psum.35 = f32[128,64]{0,1:T(8,128)S(1)} all-reduce(f32[128,64]{0,1:T(8,128)S(1)} %fusion.48), channel_id=1, replica_groups=mesh['section'=4,'expert'=4,'dp'=2] {'expert'}, use_global_device_ids=true, to_apply=%region_10.11 | all-reduce | flops 8192 | bytes 65536 | tf_op jit(solution)/shard_map/psum | solution.py:127
  113.8 9.4 %all-gather.2 = bf16[1,2048,64]{1,2,0:T(8,128)(2,1)S(1)} all-gather(bf16[1,512,64]{1,2,0:T(8,128)(2,1)S(1)} %copy-done.3), channel_id=4, replica_groups=mesh['section'=4,'expert'=4,'dp'=2] {'expert'}, dimensions={1}, use_global_device_ids=true | all-gather | bytes 327680 | tf_op jit(solution)/shard_map/all_gather | solution.py:125
  123.2 0.1 convert_reduce_fusion
  123.3 0.9 convolution_bitcast_fusion
  124.2 1.1 fusion.30
  125.3 9.5 %fusion.20 = f32[160]{0:T(256)S(1)} fusion(bf16[1,3584,2048]{2,1,0:T(8,128)(2,1)} %param.19, bf16[160,2048]{1,0:T(8,128)(2,1)S(1)} %all_gather.23, f32[160,3584]{1,0:T(8,128)} %fusion.6, f32[160,3584]{1,0:T(8,128)} %fusion.2), kind=kOutput, calls=%fused_computation.23 | convolution fusion | flops 2353233664 | bytes 19923584 | tf_op jit(solution)/shard_map/dot_general | solution.py:68
  134.9 0.1 convert_element_type.123
  135.0 2.5 %all-reduce = f32[160]{0:T(256)S(1)} all-reduce(f32[160]{0:T(256)S(1)} %fusion.20), channel_id=6, replica_groups=mesh['section'=4,'expert'=4,'dp'=2] {'dp'}, use_global_device_ids=true, to_apply=%region_12.13.clone | all-reduce | flops 160 | bytes 1280
  137.5 0.6 dynamic-slice.3
  138.7 0.2 convolution_bitcast_fusion.1
  139.0 1.3 reduce-scatter.2.cloned.1.call-done
  140.3 1.3 fusion.47
  141.6 8.9 %all-reduce.1 = (f32[128,1]{0,1:T(1,128)S(1)}, f32[128,4]{0,1:T(4,128)S(1)}) all-reduce(f32[128,1]{0,1:T(1,128)S(1)} %bitcast.140, f32[128,4]{0,1:T(4,128)S(1)} %broadcast_multiply_fusion), channel_id=1, replica_groups=mesh['section'=4,'expert'=4,'dp'=2] {'expert'}, use_global_device_ids=true, to_apply=%region_17.18 | all-reduce | flops 640 | bytes 5120 | tf_op jit(solution)/shard_map/psum | solution.py:173
  150.6 0.7 fusion.32
  151.3 0.4 fusion.28
  151.6 3.4 %collective-permute-start = (bf16[128,512]{1,0:T(8,128)(2,1)S(1)}, bf16[128,512]{1,0:T(8,128)(2,1)S(1)}, u32[]{:S(2)}, u32[]{:S(2)}) collective-permute-start(bf16[128,512]{1,0:T(8,128)(2,1)S(1)} %fusion.28), channel_id=1, source_target_pairs={{8,0},{16,8},{24,16},{0,24},{9,1},{17,9},{25,17},{1,25},{10,2},{18... | collective-permute-start | bytes 393224 | tf_op jit(solution)/shard_map/ppermute | solution.py:20
  155.1 2.5 %collective-permute-done = bf16[128,512]{1,0:T(8,128)(2,1)S(1)} collective-permute-done((bf16[128,512]{1,0:T(8,128)(2,1)S(1)}, bf16[128,512]{1,0:T(8,128)(2,1)S(1)}, u32[]{:S(2)}, u32[]{:S(2)}) %collective-permute-start) | collective-permute-done | bytes 131104 | tf_op jit(solution)/shard_map/ppermute | solution.py:20
  157.6 0.7 copy.35
  158.2 1.6 copy.36
  159.8 1.6 copy.37
  (36 shorter events, 0.4 us)
Async XLA Ops:
  8.0 90.3 %copy-start = (bf16[1,64,512]{2,1,0:T(8,128)(2,1)S(1)}, bf16[1,64,512]{2,1,0:T(8,128)(2,1)}, u32[]{:S(2)}) copy-start(bf16[1,64,512]{2,1,0:T(8,128)(2,1)} %param.21) | copy-start | bytes 196612
  8.0 17.2 %copy-start.2 = (bf16[1,128,512]{2,1,0:T(8,128)(2,1)S(1)}, bf16[1,128,512]{2,1,0:T(8,128)(2,1)}, u32[]{:S(2)}) copy-start(bf16[1,128,512]{2,1,0:T(8,128)(2,1)} %param.12) | copy-start | bytes 393220
  8.0 132.3 %reduce-scatter.2.cloned.1.call-start = ((), (), s32[]{:S(2)}) async-start(), calls=%async_computation.1 | async-start | bytes 2359296 | tf_op jit(solution)/shard_map/reduce_scatter | solution.py:159
  40.0 10.2 %copy-start.1 = (bf16[1,2048,3584]{2,1,0:T(8,128)(2,1)S(1)}, bf16[1,2048,3584]{2,1,0:T(8,128)(2,1)}, u32[]{:S(2)}) copy-start(bf16[1,2048,3584]{2,1,0:T(8,128)(2,1)} %param.18) | copy-start | bytes 44040196
  96.4 1.7 %copy-start.6 = (s32[1,4]{1,0:T(1,128)S(1)}, s32[1,4]{1,0:T(1,128)}, u32[]{:S(2)}) copy-start(s32[1,4]{1,0:T(1,128)} %param.14) | copy-start | bytes 52
  96.4 17.4 %copy-start.3 = (bf16[1,512,64]{1,2,0:T(8,128)(2,1)S(1)}, bf16[1,512,64]{1,2,0:T(8,128)(2,1)}, u32[]{:S(2)}) copy-start(bf16[1,512,64]{1,2,0:T(8,128)(2,1)} %param.20) | copy-start | bytes 196612
  98.0 59.6 %all-reduce.5.cloned.1.call-start = ((), (), s32[]{:S(2)}) async-start(), calls=%async_computation.2 | async-start | bytes 524288 | tf_op jit(solution)/shard_map/psum | solution.py:138
  125.3 9.6 %copy-start.5 = (f32[1,2048]{1,0:T(1,128)S(1)}, f32[1,2048]{1,0:T(1,128)}, u32[]{:S(2)}) copy-start(f32[1,2048]{1,0:T(1,128)} %param.15) | copy-start | bytes 24580
  125.3 12.2 %copy-start.7 = (u32[32]{0:T(128)S(1)}, u32[32]{0:T(128)}, u32[]{:S(2)}) copy-start(u32[32]{0:T(128)} %constant.94) | copy-start | bytes 388
  134.9 15.7 %copy-start.4 = (bf16[1,2048,4]{1,2,0:T(4,128)(2,1)S(1)}, bf16[1,2048,4]{1,2,0:T(4,128)(2,1)}, u32[]{:S(2)}) copy-start(bf16[1,2048,4]{1,2,0:T(4,128)(2,1)} %param.16) | copy-start | bytes 49156
  151.6 6.0 %collective-permute-start = (bf16[128,512]{1,0:T(8,128)(2,1)S(1)}, bf16[128,512]{1,0:T(8,128)(2,1)S(1)}, u32[]{:S(2)}, u32[]{:S(2)}) collective-permute-start(bf16[128,512]{1,0:T(8,128)(2,1)S(1)} %fusion.28), channel_id=1, source_target_pairs={{8,0},{16,8},{24,16},{0,24},{9,1},{17,9},{25,17},{1,25},{10,2},{18... | collective-permute-start | bytes 393224 | tf_op jit(solution)/shard_map/ppermute | solution.py:20
Sparse Core Ops, SparseCore 0:
  98.1 42.1 reduce-scatter.1
Sparse Core Ops, SparseCore 1:
  125.4 18.3 all-reduce.4
where the time goes:
time: 169 us
  matrix products  66.8 us (40%)
  blocking collectives  66 us (39%)
  between operations  16.4 us (10%)
  local copies, waits for them, and re-layouts  9.96 us (6%)
  waiting for transfers between devices  3.87 us (2%)
  starting transfers between devices  3.51 us (2%)
  other arithmetic  2.28 us (1%)
    psum x1, blocking collectives, body(): lax.psum(jnp.dot(gradient_columns, backward_columns.T, preferred_element_...  15.4 us
    dot_general x1, matrix products, expert_back(): jnp.dot(d_up, expert_up_weight.T, preferred_element_type=jnp.float32)  12.7 us
    dot_general x1, matrix products, expert_back(): jnp.dot(d_gate, expert_gate_weight.T, preferred_element_type=jnp.float32)  12.1 us
    all_gather x1, blocking collectives, body(): lax.all_gather(s_cols, 'expert', axis=1, tiled=True)  12 us
    dot_general x1, matrix products, expert_back(): jnp.dot(adapter_gradient_list, expert_down_weight.T, preferred_element_ty...  11.6 us
    all_gather x1, blocking collectives, body(): lax.all_gather(gradient_columns, 'expert', axis=1, tiled=True)  9.67 us
    dot_general x1, matrix products, expert_back(): jnp.dot(hidden, expert_down_weight, preferred_element_type=jnp.float32)  9.53 us
    all_gather x1, blocking collectives, body(): a_full = lax.all_gather(down_map_rows, 'expert', axis=0, tiled=True)  9.38 us
  transfers between devices with their start and end apart: 3, of which 2 were waited for; matrix products, arithmetic and copies ran while one was open for 9% of the time, Pallas kernels for 0%

commit v1 on v0

v1 whole, which is shorter than its diff:
```python
import functools

import jax
import jax.numpy as jnp
from jax import lax
from jax.experimental import pallas as pl
from jax.experimental.pallas import tpu as pltpu
from jax.sharding import PartitionSpec as P

ADAPTER_RANK = 16
CAP = 80

EPS = 1e-05
ADAPTER_SCALE = 0.5
MESH = pl.DeviceIdType.MESH
VMEM_LIMIT = 60 * 1024 * 1024
LANES = 128
LAST = (((1,), (1,)), ((), ()))
FIRST = (((0,), (0,)), ((), ()))


def job_columns(job_token_lengths, offset, count):
    ends = jnp.cumsum(job_token_lengths, dtype=jnp.int32)
    position = offset + jnp.arange(count, dtype=jnp.int32)
    owner = jnp.sum((ends[None, :] <= position[:, None]).astype(jnp.int32), axis=1, dtype=jnp.int32)
    column_owner = (
        jnp.arange(job_token_lengths.shape[0] * ADAPTER_RANK, dtype=jnp.int32) // ADAPTER_RANK
    )
    return (owner[:, None] == column_owner[None, :]).astype(jnp.float32)


def greet(targets):
    barrier = pltpu.get_barrier_semaphore()
    for target in targets:
        pl.semaphore_signal(barrier, inc=1, device_id=target, device_id_type=MESH)
    pl.semaphore_wait(barrier, len(targets))


def gather_kernel(
    n, per, rows_ref, stats_ref, lows_ref, rows_out, stats_out, lows_out,
    rs, rr, ss, sr, ls, lr, fs, fr, own,
):
    me = lax.axis_index("expert")
    core = lax.axis_index("dp")
    partner = {"dp": 1 - core}
    peers = [lax.rem(me + k, n) for k in range(1, n)]
    greet([{"expert": peer} for peer in peers] + [partner])

    def send(src, dst, a, b, k, target):
        copy = pltpu.make_async_remote_copy(
            src_ref=src, dst_ref=dst, send_sem=a.at[k], recv_sem=b.at[k],
            device_id=target, device_id_type=MESH,
        )
        copy.start()
        return copy

    rows, small = [], []
    for k, peer in enumerate(peers):
        target = {"expert": peer}
        rows.append(send(rows_ref.at[peer // per], rows_out.at[core, me], rs, rr, k, target))
        small.append(send(stats_ref, stats_out.at[me], ss, sr, k, target))
        small.append(send(lows_ref, lows_out.at[me], ls, lr, k, target))
    mine = rows_ref.at[me // per]
    local = [
        pltpu.make_async_copy(mine, rows_out.at[core, me], own.at[0]),
        pltpu.make_async_copy(stats_ref, stats_out.at[me], own.at[1]),
        pltpu.make_async_copy(lows_ref, lows_out.at[me], own.at[2]),
    ]
    for copy in local:
        copy.start()
    passed = [send(mine, rows_out.at[core, me], fs, fr, n - 1, partner)]
    for k in range(n - 1):
        rows[k].wait_recv()
        origin = lax.rem(me + (n - 1 - k), n)
        landed = rows_out.at[core, origin]
        passed.append(send(landed, landed, fs, fr, k, partner))
    for copy in rows:
        copy.wait_send()
    for copy in small + local + passed:
        copy.wait()


def gather(n, per, shards, rows, stats, lows):
    vmem = pl.BlockSpec(memory_space=pltpu.VMEM)
    dma = pltpu.SemaphoreType.DMA
    return pl.pallas_call(
        functools.partial(gather_kernel, n, per),
        out_shape=(
            jax.ShapeDtypeStruct((shards, n) + rows.shape[1:], rows.dtype),
            jax.ShapeDtypeStruct((n,) + stats.shape, stats.dtype),
            jax.ShapeDtypeStruct((n,) + lows.shape, lows.dtype),
        ),
        in_specs=[vmem] * 3,
        out_specs=(vmem,) * 3,
        scratch_shapes=[dma((n - 1,))] * 6 + [dma((n,))] * 2 + [dma((3,))],
        compiler_params=pltpu.CompilerParams(
            collective_id=0, has_side_effects=True, vmem_limit_bytes=VMEM_LIMIT
        ),
    )(rows, stats, lows)


def expert_kernel(
    n, width, rows_ref, gain_ref, wg_ref, wu_ref, wd_ref, dn_ref, vec_ref, normed, cot, acc, vec
):
    step = pl.program_id(0)
    shards, cap = rows_ref.shape[0], rows_ref.shape[2]

    @pl.when(step == 0)
    def _():
        for s in range(shards):
            r = slice(s * cap, (s + 1) * cap)
            total = jnp.zeros((cap, 1), jnp.float32)
            for j in range(n):
                x = rows_ref[s, j, :, :width].astype(jnp.float32)
                total += jnp.sum(x * x, axis=1, keepdims=True)
            scale = lax.rsqrt(total / (n * width) + EPS)
            for j in range(n):
                c = slice(j * width, (j + 1) * width)
                x = rows_ref[s, j, :, :width].astype(jnp.float32)
                normed[r, c] = (x * scale * gain_ref[:, c]).astype(jnp.bfloat16)
                cot[r, c] = rows_ref[s, j, :, width:]
        acc[...] = jnp.zeros_like(acc)
        vec[...] = jnp.zeros_like(vec)

    x, g = normed[...], cot[...]
    gate = jnp.dot(x, wg_ref[...], preferred_element_type=jnp.float32)
    up = jnp.dot(x, wu_ref[...], preferred_element_type=jnp.float32)
    back = lax.dot_general(g, wd_ref[...], LAST, preferred_element_type=jnp.float32)
    sig = jax.nn.sigmoid(gate)
    act = gate * sig
    d_up = back * act
    d_gate = back * up * sig * (1.0 + gate * (1.0 - sig))
    gate_term = jnp.sum(d_up * up, axis=1, keepdims=True)
    stat_term = jnp.sum(d_gate * gate + d_up * up, axis=1, keepdims=True)
    lane = lax.broadcasted_iota(jnp.int32, vec.shape, 1)
    vec[...] += jnp.where(lane % 2 == 0, gate_term, stat_term)
    acc[...] += lax.dot_general(
        d_gate.astype(jnp.bfloat16), wg_ref[...], LAST, preferred_element_type=jnp.float32
    ) + lax.dot_general(
        d_up.astype(jnp.bfloat16), wu_ref[...], LAST, preferred_element_type=jnp.float32
    )

    @pl.when(step == pl.num_programs(0) - 1)
    def _():
        for s in range(shards):
            r = slice(s * cap, (s + 1) * cap)
            vec_ref[s] = vec[r, :]
            for j in range(n):
                dn_ref[s, j] = acc[r, j * width:(j + 1) * width]


def expert_back(rows, gains, wg, wu, wd):
    shards, n, cap, double = rows.shape
    width = double // 2
    model, hidden = n * width, wg.shape[2]
    tile = next(t for t in (512, 256, 128, hidden) if hidden % t == 0)
    slots = shards * cap
    return pl.pallas_call(
        functools.partial(expert_kernel, n, width),
        grid=(hidden // tile,),
        out_shape=(
            jax.ShapeDtypeStruct((shards, n, cap, width), jnp.float32),
            jax.ShapeDtypeStruct((shards, cap, LANES), jnp.float32),
        ),
        in_specs=[
            pl.BlockSpec(rows.shape, lambda i: (0, 0, 0, 0)),
            pl.BlockSpec((1, model), lambda i: (0, 0)),
            pl.BlockSpec((None, model, tile), lambda i: (0, 0, i)),
            pl.BlockSpec((None, model, tile), lambda i: (0, 0, i)),
            pl.BlockSpec((None, tile, model), lambda i: (0, i, 0)),
        ],
        out_specs=(
            pl.BlockSpec((shards, n, cap, width), lambda i: (0, 0, 0, 0)),
            pl.BlockSpec((shards, cap, LANES), lambda i: (0, 0, 0)),
        ),
        scratch_shapes=[
            pltpu.VMEM((slots, model), jnp.bfloat16),
            pltpu.VMEM((slots, model), jnp.bfloat16),
            pltpu.VMEM((slots, model), jnp.float32),
            pltpu.VMEM((slots, LANES), jnp.float32),
        ],
        compiler_params=pltpu.CompilerParams(
            dimension_semantics=("arbitrary",), vmem_limit_bytes=VMEM_LIMIT
        ),
    )(rows, gains, wg, wu, wd)


def scatter_kernel(
    n, per, experts, sections,
    dn_ref, vec_ref, pd_ref, pu_ref, st_ref, tok_ref, base_ref, x_ref, g_ref, gain_ref, rt_ref,
    back_out, pd_out, pu_out,
    pdn, pvec, ppd, ppu, sendbuf, landing, result, ps, pr, qs, qr, es, er, zs, zr,
):
    me = lax.axis_index("expert")
    core = lax.axis_index("dp")
    sec = lax.axis_index("section")
    other = 1 - core
    partner = {"dp": other}
    width = x_ref.shape[1]
    ahead = {"section": lax.rem(sec + sections - 1, sections)}
    behind = {"section": lax.rem(sec + 1, sections)}
    peers = [lax.rem(me + k, n) for k in range(1, n)]
    greet([{"expert": peer} for peer in peers] + [partner, ahead, behind])

    def send(src, dst, a, b, k, target):
        copy = pltpu.make_async_remote_copy(
            src_ref=src, dst_ref=dst, send_sem=a.at[k], recv_sem=b.at[k],
            device_id=target, device_id_type=MESH,
        )
        copy.start()
        return copy

    shared = [send(vec_ref.at[other], pvec, qs, qr, 0, partner)]
    blocks = [
        send(dn_ref.at[other, peer], pdn.at[k], ps, pr, k, partner)
        for k, peer in enumerate(peers + [me])
    ]
    shared.append(send(pd_ref, ppd, qs, qr, 1, partner))
    shared.append(send(pu_ref, ppu, qs, qr, 2, partner))

    shared[0].wait()
    v = vec_ref[core] + pvec[...]
    high = v.astype(jnp.bfloat16)
    rest = (v - high.astype(jnp.float32)).astype(jnp.bfloat16)
    lane = lax.broadcasted_iota(jnp.int32, v.shape, 1)
    packed = jnp.where(lane < 2, high.astype(jnp.float32), rest.astype(jnp.float32)).astype(
        jnp.bfloat16
    )
    sent = []
    for k, peer in enumerate(peers):
        blocks[k].wait()
        sendbuf[k, :, :width] = (dn_ref[core, peer] + pdn[k]).astype(jnp.bfloat16)
        sendbuf[k, :, width:] = packed
        sent.append(send(sendbuf.at[k], landing.at[k], es, er, k, {"expert": peer}))
    blocks[n - 1].wait()
    own_rows = (dn_ref[core, me] + pdn[n - 1]).astype(jnp.bfloat16)

    token = tok_ref[...]
    column = lambda i: token[:, i:i + 1]
    spread = jnp.zeros_like(column(0))
    stat = jnp.zeros_like(spread)
    total = base_ref[...]

    def pick(ref_index, values):
        return jnp.dot(st_ref[ref_index], values, preferred_element_type=jnp.float32)

    def weights_of(expert):
        gate, sign = jnp.zeros_like(spread), jnp.zeros_like(spread)
        for e in range(experts):
            mark = (expert == e).astype(jnp.float32)
            gate += mark * column(e)
            sign += mark * column(experts + e)
        return gate, sign

    def add(expert, row_part, vec_part, total, spread, stat):
        gate, sign = weights_of(expert)
        picked = pick(expert, vec_part)
        spread = spread + sign * (picked[:, 0:1] + picked[:, 2:3])
        stat = stat + gate * (picked[:, 1:2] + picked[:, 3:4])
        return total + gate * pick(expert, row_part), spread, stat

    total, spread, stat = add(me // per, own_rows, packed, total, spread, stat)
    for k in range(n - 1):
        sent[k].wait()
        expert = lax.rem(me + (n - 1 - k), n) // per
        total, spread, stat = add(
            expert, landing[k, :, :width], landing[k, :, width:], total, spread, stat
        )
    scale = column(2 * experts + 1)
    delta = spread * column(2 * experts)
    for e in range(experts):
        total = total + (delta * column(experts + e)) * rt_ref[e:e + 1, :]
    stat = stat / scale + column(2 * experts + 2) + delta * column(2 * experts + 3)
    x = x_ref[...].astype(jnp.float32)
    g = g_ref[...].astype(jnp.float32)
    weighted = total * gain_ref[...]
    out = g + scale * weighted - x * (scale * scale * scale * stat / (n * width))
    result[...] = out.astype(jnp.bfloat16)
    handed = send(result, back_out, zs, zr, 0, ahead)
    shared[1].wait()
    pd_out[...] = pd_ref[...] + ppd[...]
    shared[2].wait()
    pu_out[...] = pu_ref[...] + ppu[...]
    handed.wait()


def scatter(n, per, experts, sections, dn, vec, pd, pu, *rest):
    cap, width = dn.shape[2:]
    x = rest[3]
    vmem = pl.BlockSpec(memory_space=pltpu.VMEM)
    dma = pltpu.SemaphoreType.DMA
    return pl.pallas_call(
        functools.partial(scatter_kernel, n, per, experts, sections),
        out_shape=(
            jax.ShapeDtypeStruct(x.shape, jnp.bfloat16),
            jax.ShapeDtypeStruct(pd.shape, jnp.float32),
            jax.ShapeDtypeStruct(pu.shape, jnp.float32),
        ),
        in_specs=[vmem] * (4 + len(rest)),
        out_specs=(vmem,) * 3,
        scratch_shapes=[
            pltpu.VMEM((n, cap, width), jnp.float32),
            pltpu.VMEM(vec.shape[1:], jnp.float32),
            pltpu.VMEM(pd.shape, jnp.float32),
            pltpu.VMEM(pu.shape, jnp.float32),
            pltpu.VMEM((n - 1, cap, width + LANES), jnp.bfloat16),
            pltpu.VMEM((n - 1, cap, width + LANES), jnp.bfloat16),
            pltpu.VMEM(x.shape, jnp.bfloat16),
            dma((n,)), dma((n,)), dma((3,)), dma((3,)),
            dma((n - 1,)), dma((n - 1,)), dma((1,)), dma((1,)),
        ],
        compiler_params=pltpu.CompilerParams(
            collective_id=1, has_side_effects=True, vmem_limit_bytes=VMEM_LIMIT
        ),
    )(dn, vec, pd, pu, *rest)


def body(
    stash,
    cotangent,
    backward_expert_routes,
    backward_job_lengths,
    layer_norm_gains,
    router,
    expert_gate_weight,
    expert_up_weight,
    expert_down_weight,
    adapter_down_maps,
    adapter_up_maps,
):
    n = lax.axis_size("expert")
    shards = lax.axis_size("dp")
    sections = lax.axis_size("section")
    experts = router.shape[2]
    per = n // experts
    me = lax.axis_index("expert")
    x, g = stash[0], cotangent[0]
    count, width = x.shape
    routes = backward_expert_routes[0]
    gain = lax.dynamic_slice_in_dim(layer_norm_gains, me * width, width, 1)
    route_cols = lax.dynamic_slice_in_dim(router[0], me * width, width, 0)
    down, up_map = adapter_down_maps[0], adapter_up_maps[0]
    ranks = down.shape[1]

    labels = jnp.arange(experts, dtype=jnp.int32)
    first = (routes[:, 0:1] == labels[None, :]).astype(jnp.float32)
    second = (routes[:, 1:2] == labels[None, :]).astype(jnp.float32)
    member = first + second
    order = jnp.arange(count, dtype=jnp.int32)
    before = (order[None, :] < order[:, None]).astype(jnp.bfloat16)
    rank = jnp.dot(before, member.astype(jnp.bfloat16), preferred_element_type=jnp.float32)
    place = jnp.where(member > 0, rank, -1.0)
    slots = jnp.arange(CAP, dtype=jnp.float32)
    spread_to = (place.T[:, :, None] == slots[None, None, :]).astype(jnp.bfloat16)
    select = (place.T[:, None, :] == slots[None, :, None]).astype(jnp.bfloat16)

    both = jnp.concatenate([x, g], axis=1)
    rows = jnp.dot(
        select.reshape(experts * CAP, count), both, preferred_element_type=jnp.float32
    ).astype(jnp.bfloat16).reshape(experts, CAP, 2 * width)
    xf = x.astype(jnp.float32)
    gained = (xf * gain).astype(jnp.bfloat16)
    square = jnp.sum(xf * xf, axis=1)[None, :]
    raw = lax.dot_general(
        route_cols, gained, (((0,), (1,)), ((), ())), preferred_element_type=jnp.float32
    )
    fill = -(1 + experts) % 8
    stats = jnp.concatenate([square, raw, jnp.zeros((fill, count), jnp.float32)], axis=0)
    lows = jnp.concatenate(
        [
            jnp.dot(gained, down, preferred_element_type=jnp.float32),
            lax.dot_general(g, up_map, LAST, preferred_element_type=jnp.float32),
        ],
        axis=1,
    ).astype(jnp.bfloat16)

    all_rows, all_stats, all_lows = gather(n, per, shards, rows, stats, lows)

    dn, vec = expert_back(
        all_rows, layer_norm_gains, expert_gate_weight, expert_up_weight, expert_down_weight
    )

    stat = jnp.sum(all_stats, axis=0).T
    scale = lax.rsqrt(stat[:, 0:1] / (n * width) + EPS)
    raw_logits = stat[:, 1:1 + experts]
    sign = first - second
    raw_spread = jnp.sum(sign * raw_logits, axis=1, keepdims=True)
    upper = jax.nn.sigmoid(raw_spread * scale)
    table = upper * first + (1.0 - upper) * second
    low_all = jnp.sum(all_lows.astype(jnp.float32), axis=0)
    raw_low, g_low = low_all[:, :ranks], low_all[:, ranks:]
    mask = job_columns(backward_job_lengths[0], lax.axis_index("dp") * count, count)
    low = (raw_low * scale * mask).astype(jnp.bfloat16)
    d_low = (ADAPTER_SCALE * g_low * mask).astype(jnp.bfloat16)
    normed_cols = (xf * scale * gain).astype(jnp.bfloat16)
    pu = ADAPTER_SCALE * lax.dot_general(low, g, FIRST, preferred_element_type=jnp.float32)
    pd = lax.dot_general(normed_cols, d_low, FIRST, preferred_element_type=jnp.float32)
    base = lax.dot_general(d_low, down, LAST, preferred_element_type=jnp.float32)
    low_stat = jnp.sum(d_low.astype(jnp.float32) * raw_low, axis=1, keepdims=True)
    columns = [table, sign, upper * (1.0 - upper), scale, low_stat, raw_spread]
    used = sum(c.shape[1] for c in columns)
    token = jnp.concatenate(columns + [jnp.zeros((count, -used % LANES), jnp.float32)], axis=1)

    handed_back, down_grad, up_grad = scatter(
        n, per, experts, sections, dn, vec, pd, pu,
        spread_to, token, base, x, g, gain, route_cols.astype(jnp.float32).T,
    )
    return (handed_back[None], down_grad[None], up_grad[None])


def solution(mesh):
    return jax.shard_map(
        body,
        mesh=mesh,
        in_specs=(
            P("section", "dp", "expert"),
            P("section", "dp", "expert"),
            P("section", "dp", None),
            P("section", None),
            P("section", None),
            P("section", None, None),
            P("section", None, ("expert", "dp")),
            P("section", None, ("expert", "dp")),
            P("section", ("expert", "dp"), None),
            P("section", "expert", None),
            P("section", None, "expert"),
        ),
        out_specs=(
            P("section", "dp", "expert"),
            P("section", "expert", None),
            P("section", None, "expert"),
        ),
        check_vma=False,
    )
```

time: 169 us -> 84.9 us (0.50)
  blocking collectives: 66 us -> 0 us
  Pallas kernels: 0 us -> 61.8 us
  matrix products: 66.8 us -> 8.38 us
  between operations: 16.4 us -> 0.83 us
  waiting for transfers between devices: 3.87 us -> 0 us
  starting transfers between devices: 3.51 us -> 0 us
  other arithmetic: 2.28 us -> 5.63 us
  local copies, waits for them, and re-layouts: 9.96 us -> 7.86 us
    pallas_call x0 -> x3, Pallas kernels: none -> 61.8 us  [the longest x1 26.6 us: expert_back(): pl.pallas_call(functools.partial(expert_kernel, n, width), grid=(hidden /...]
    dot_general x17 -> x8, matrix products: 66.8 us -> 8.38 us  [the longest x1 2.12 us: body(): jnp.dot(select.reshape(experts * CAP, count), both, preferred_element_typ...]
    all_gather x7 -> x0, blocking collectives: 39.2 us -> none  [the longest x1 12 us: body(): lax.all_gather(s_cols, 'expert', axis=1, tiled=True)]
    psum x2 -> x0, blocking collectives: 24.3 us -> none  [the longest x1 15.4 us: body(): lax.psum(jnp.dot(gradient_columns, backward_columns.T, preferred_element_...]
    ppermute x1 -> x0, starting transfers between devices: 3.43 us -> none  [from_behind(): return lax.ppermute(block, axis, route)]
    ppermute x1 -> x0, waiting for transfers between devices: 2.52 us -> none  [from_behind(): return lax.ppermute(block, axis, route)]
    unnamed x1 -> x0, blocking collectives: 2.47 us -> none
    reshape x1 -> x0, local copies, waits for them, and re-layouts: 2.18 us -> none  [body(): dn_slots.reshape(shards, CAP, groups, width)]
  transfers between devices with their start and end apart: 3 -> 0, of which waited for: 2 -> 0; matrix products, arithmetic and copies ran while one was open for 9% -> 0% of each run, Pallas kernels for 0% -> 0%
where the time goes in v1:
time: 84.9 us; the launch traced here: 84.5 us
  Pallas kernels  61.8 us (73%)
  matrix products  8.38 us (10%)
  local copies, waits for them, and re-layouts  7.86 us (9%)
  other arithmetic  5.63 us (7%)
    pallas_call x1, Pallas kernels, expert_back(): pl.pallas_call(functools.partial(expert_kernel, n, width), grid=(hidden /...  26.6 us
    pallas_call x1, Pallas kernels, scatter(): pl.pallas_call(functools.partial(scatter_kernel, n, per, experts, section...  18.4 us
    pallas_call x1, Pallas kernels, gather(): pl.pallas_call(functools.partial(gather_kernel, n, per), out_shape=(jax.S...  16.9 us
    unnamed x17, local copies, waits for them, and re-layouts  4.9 us
    dot_general x1, matrix products, body(): jnp.dot(select.reshape(experts * CAP, count), both, preferred_element_typ...  2.12 us

profile of v1, /device:TPU:0, one launch (start us, length us, event | category | flops | bytes accessed | tf_op | source)
XLA Modules:
  0.0 84.5 jit_solution(10674263707523819413)
XLA Ops:
  0.6 0.0 copy-start
  0.7 0.1 eq.107
  0.7 0.8 slice_bitcast_fusion.1
  1.5 0.2 convolution_select_fusion
  1.7 0.1 bitcast_compare_fusion
  1.9 2.1 %convolution_convert_fusion = bf16[320,1024]{1,0:T(8,128)(2,1)} fusion(pred[320,128]{1,0:T(32,128)(4,1)S(1)} %bitcast_compare_fusion, bf16[128,512]{1,0:T(8,128)(2,1)} %bitcast.53, bf16[128,512]{1,0:T(8,128)(2,1)} %bitcast.50), kind=kOutput, calls=%fused_computation | convolution fusion | flops 84738048 | bytes 958464 | tf_op jit(solution)/shard_map/dot_general | solution.py:358
  4.0 0.7 constant_dynamic-slice_fusion.gain_ref
  4.7 1.1 %fusion.13 = f32[4,128]{1,0:T(4,128)S(1)} fusion(bf16[1,128,512]{2,1,0:T(8,128)(2,1)} %param.11, f32[512]{0:T(512)S(1)} %bitcast.60, bf16[1,2048,4]{1,2,0:T(4,128)(2,1)} %param.16, s32[]{:T(128)S(6)} %select_n.19), kind=kOutput, calls=%fused_computation.22 | convolution fusion | flops 720896 | bytes 139268 | tf_op jit(solution)/shard_map/dot_general | solution.py:364
  5.7 1.0 %fusion = f32[128]{0:T(128)S(1)} fusion(bf16[1,128,512]{2,1,0:T(8,128)(2,1)} %param.11), kind=kLoop, calls=%fused_computation.7 | loop fusion | flops 196480 | bytes 131584 | tf_op jit(solution)/shard_map/reduce_sum | solution.py:363
  6.8 0.1 pad.4.clone
  6.9 0.7 maximum_maximum_fusion.stats_ref
  7.5 1.1 %convolution_convert_fusion.1 = bf16[128,64]{0,1:T(8,128)(2,1)S(1)} fusion(bf16[1,64,512]{2,1,0:T(8,128)(2,1)} %param.21, bf16[1,128,512]{2,1,0:T(8,128)(2,1)} %param.12), kind=kOutput, calls=%fused_computation.2 | convolution fusion | flops 8396800 | bytes 212992 | tf_op jit(solution)/shard_map/dot_general | solution.py:372
  8.6 0.1 copy.54
  8.7 0.0 copy-done
  8.7 1.1 %convolution_convert_fusion.2 = bf16[128,64]{0,1:T(8,128)(2,1)S(1)} fusion(bf16[1,128,512]{2,1,0:T(8,128)(2,1)} %param.11, f32[512]{0:T(512)S(1)} %bitcast.61, bf16[1,512,64]{1,2,0:T(8,128)(2,1)S(1)} %copy-done), kind=kOutput, calls=%fused_computation.3 | convolution fusion | flops 8593408 | bytes 215040 | tf_op jit(solution)/shard_map/dot_general | solution.py:371
  9.8 0.1 copy.53
  9.9 0.7 pad_maximum_fusion.lows_ref
  10.6 16.9 %shard_map.130 = (bf16[2,4,80,1024]{3,2,1,0:T(8,128)(2,1)}, f32[4,8,128]{2,1,0:T(8,128)}, bf16[4,128,128]{2,1,0:T(8,128)(2,1)}) custom-call(bf16[4,80,1024]{2,1,0:T(8,128)(2,1)} %bitcast.52, f32[8,128]{1,0:T(8,128)} %maximum_maximum_fusion.stats_ref, bf16[128,128]{1,0:T(8,128)(2,1)} %pad_maximum_fusion.lows_ref), custom_call_target="tpu_custom_call" | custom-call | tf_op jit(solution)/shard_map/pallas_call | solution.py:86
  27.5 0.0 copy-start.3
  27.5 0.0 copy-start.6
  27.5 0.0 copy-start.5
  27.5 0.0 copy-start.1
  27.6 0.0 copy-start.2
  27.6 26.6 %shard_map.131 = (f32[2,4,80,512]{3,2,1,0:T(8,128)}, f32[2,80,128]{2,1,0:T(8,128)}) custom-call(bf16[2,4,80,1024]{3,2,1,0:T(8,128)(2,1)} %get-tuple-element.11.rows_ref, f32[1,2048]{1,0:T(1,128)} %gain_ref.1, bf16[1,2048,3584]{2,1,0:T(8,128)(2,1)} %wg_ref.1, bf16[1,2048,3584]{2,1,0:T(8,128)(2,1)} %wu_ref.1, bf16[1,3584,2048]{2,1,0:T(8,128)(2,1)} %wd_ref.1), custom_call_target="tpu_custom_call" | custom-call | tf_op jit(solution)/shard_map/pallas_call | solution.py:158
  54.1 0.0 copy-done.3
  54.2 0.0 copy-done.6
  54.2 0.2 reduce-window.8
  54.4 0.1 convert_reduce_fusion.1
  54.5 0.2 multiply_reduce_fusion
  54.6 0.0 copy-done.5
  54.7 0.1 copy.55
  54.8 0.2 fusion.18
  55.0 0.1 copy.57
  55.1 0.1 fusion.20
  55.2 1.0 %fusion.8.pd_ref = f32[512,64]{1,0:T(8,128)} fusion(bf16[128,64]{1,0:T(8,128)(2,1)S(1)} %get-tuple-element.40, f32[512]{0:T(512)S(1)} %bitcast.62, f32[128]{0:T(128)S(1)} %get-tuple-element.44, bf16[1,128,512]{2,1,0:T(8,128)(2,1)S(1)} %copy-done.1), kind=kOutput, calls=%fused_computation.19 | convolution fusion | flops 8650752 | bytes 281088 | tf_op jit(solution)/shard_map/dot_general | solution.py:397
  56.2 0.0 copy-done.2
  56.2 0.9 %convolution_multiply_fusion.pu_ref = f32[64,512]{1,0:T(8,128)} fusion(f32[128,128]{1,0:T(8,128)S(1)} %convert_reduce_fusion, f32[128]{0:T(128)S(1)} %get-tuple-element.44, s32[64]{0:T(128)S(1)} %and_select_fusion, s32[128]{0:T(128)S(1)} %convert_reduce_fusion.1, bf16[1,128,512]{2,1,0:T(8,128)(2,1)S(1)} %copy-done.2), kind=kOutput, calls=%fused_computation.1 | convolution fusion | flops 8454144 | bytes 328960 | tf_op jit(solution)/shard_map/dot_general | solution.py:396
  57.2 0.8 fusion.6.st_ref
  57.9 0.1 fusion.42
  58.1 0.1 convert_subtract_fusion
  58.2 0.1 copy.59
  58.3 0.8 concatenate.16.tok_ref
  59.1 0.9 %fusion.22.base_ref = f32[128,512]{1,0:T(8,128)} fusion(bf16[128,64]{1,0:T(8,128)(2,1)S(1)} %get-tuple-element.40, bf16[1,512,64]{1,2,0:T(8,128)(2,1)S(1)} %copy-done), kind=kOutput, calls=%fused_computation.39 | convolution fusion | flops 8388608 | bytes 344064 | tf_op jit(solution)/shard_map/dot_general | solution.py:398
  60.0 1.3 %convert_bitcast_fusion.rt_ref = f32[4,512]{1,0:T(4,128)} fusion(bf16[1,2048,4]{1,2,0:T(4,128)(2,1)} %param.16, s32[]{:T(128)S(6)} %select_n.19), kind=kLoop, calls=%fused_computation.55 | loop fusion | flops 2048 | bytes 12292 | tf_op jit(solution)/shard_map/transpose | solution.py:406
  61.3 18.4 %shard_map.132 = (bf16[128,512]{1,0:T(8,128)(2,1)}, f32[512,64]{1,0:T(8,128)}, f32[64,512]{1,0:T(8,128)}) custom-call(f32[2,4,80,512]{3,2,1,0:T(8,128)} %get-tuple-element.12.dn_ref, f32[2,80,128]{2,1,0:T(8,128)} %get-tuple-element.13.vec_ref, f32[512,64]{1,0:T(8,128)} %fusion.8.pd_ref, f32[64,512]{1,0:T(8,128)} %convolution_multiply_fusion.pu_ref, ...), custom_call_target="tpu_custom_call" | custom-call | tf_op jit(solution)/shard_map/pallas_call | solution.py:292
  79.7 1.7 %copy.62 = f32[1,512,64]{1,2,0:T(8,128)} copy(f32[1,512,64]{2,1,0:T(8,128)} %bitcast.57) | data formatting | bytes 262144
  81.4 1.6 %copy.69 = bf16[1,128,512]{2,1,0:T(8,128)(2,1)} copy(bf16[1,128,512]{2,1,0:T(8,128)(2,1)} %bitcast.59) | data formatting | bytes 262144
  82.9 1.6 %copy.70 = f32[1,64,512]{2,1,0:T(8,128)} copy(f32[1,64,512]{2,1,0:T(8,128)} %bitcast.58) | data formatting | bytes 262144
  (10 shorter events, 0.1 us)
Async XLA Ops:
  0.6 8.1 %copy-start = (bf16[1,512,64]{1,2,0:T(8,128)(2,1)S(1)}, bf16[1,512,64]{1,2,0:T(8,128)(2,1)}, u32[]{:S(2)}) copy-start(bf16[1,512,64]{1,2,0:T(8,128)(2,1)} %param.20) | copy-start | bytes 196612
  4.7 50.5 %copy-start.4 = (f32[1,512]{1,0:T(1,128)}, f32[1,512]{1,0:T(1,128)S(1)}, u32[]{:S(2)}) copy-start(f32[1,512]{1,0:T(1,128)S(1)} %constant_dynamic-slice_fusion.gain_ref) | copy-start | bytes 6148
  27.5 26.6 %copy-start.3 = (bf16[4,128,128]{2,1,0:T(8,128)(2,1)S(1)}, bf16[4,128,128]{2,1,0:T(8,128)(2,1)}, u32[]{:S(2)}) copy-start(bf16[4,128,128]{2,1,0:T(8,128)(2,1)} %get-tuple-element.15) | copy-start | bytes 393220
  27.5 26.7 %copy-start.6 = (s32[1,4]{1,0:T(1,128)S(1)}, s32[1,4]{1,0:T(1,128)}, u32[]{:S(2)}) copy-start(s32[1,4]{1,0:T(1,128)} %param.14) | copy-start | bytes 52
  27.5 27.1 %copy-start.5 = (f32[4,8,128]{2,1,0:T(8,128)S(1)}, f32[4,8,128]{2,1,0:T(8,128)}, u32[]{:S(2)}) copy-start(f32[4,8,128]{2,1,0:T(8,128)} %get-tuple-element.14) | copy-start | bytes 49156
  27.5 27.7 %copy-start.1 = (bf16[1,128,512]{2,1,0:T(8,128)(2,1)S(1)}, bf16[1,128,512]{2,1,0:T(8,128)(2,1)}, u32[]{:S(2)}) copy-start(bf16[1,128,512]{2,1,0:T(8,128)(2,1)} %param.11) | copy-start | bytes 393220
  27.6 28.7 %copy-start.2 = (bf16[1,128,512]{2,1,0:T(8,128)(2,1)S(1)}, bf16[1,128,512]{2,1,0:T(8,128)(2,1)}, u32[]{:S(2)}) copy-start(bf16[1,128,512]{2,1,0:T(8,128)(2,1)} %param.12) | copy-start | bytes 393220

commit v2 on v1

--- a/solution.py
+++ b/solution.py
@@ -37,8 +37,8 @@
 
 
 def gather_kernel(
-    n, per, rows_ref, stats_ref, lows_ref, rows_out, stats_out, lows_out,
-    rs, rr, ss, sr, ls, lr, fs, fr, own,
+    n, per, select_ref, x_ref, g_ref, gain_ref, route_ref, down_ref, up_ref,
+    rows_out, stats_out, lows_out, rows_ref, stats_ref, lows_ref, rs, rr, ss, sr, ls, lr, fs, fr, own,
 ):
     me = lax.axis_index("expert")
     core = lax.axis_index("dp")
@@ -54,10 +54,38 @@
         copy.start()
         return copy
 
+    width = x_ref.shape[1]
+    x, g = x_ref[...], g_ref[...]
+    for e in range(select_ref.shape[0]):
+        chosen = select_ref[e]
+        rows_ref[e, :, :width] = jnp.dot(chosen, x, preferred_element_type=jnp.float32).astype(
+            jnp.bfloat16
+        )
+        rows_ref[e, :, width:] = jnp.dot(chosen, g, preferred_element_type=jnp.float32).astype(
+            jnp.bfloat16
+        )
     rows, small = [], []
     for k, peer in enumerate(peers):
         target = {"expert": peer}
         rows.append(send(rows_ref.at[peer // per], rows_out.at[core, me], rs, rr, k, target))
+    xf = x.astype(jnp.float32)
+    gained = (xf * gain_ref[...]).astype(jnp.bfloat16)
+    raw = lax.dot_general(route_ref[...], gained, LAST, preferred_element_type=jnp.float32)
+    square = lax.dot_general(
+        jnp.ones(route_ref.shape, jnp.float32), xf * xf, LAST,
+        precision=lax.Precision.HIGHEST, preferred_element_type=jnp.float32,
+    )
+    line = lax.broadcasted_iota(jnp.int32, raw.shape, 0)
+    stats_ref[...] = jnp.where(line == 0, square, raw)
+    lows_ref[...] = jnp.concatenate(
+        [
+            jnp.dot(gained, down_ref[...], preferred_element_type=jnp.float32),
+            lax.dot_general(g, up_ref[...], LAST, preferred_element_type=jnp.float32),
+        ],
+        axis=1,
+    ).astype(jnp.bfloat16)
+    for k, peer in enumerate(peers):
+        target = {"expert": peer}
         small.append(send(stats_ref, stats_out.at[me], ss, sr, k, target))
         small.append(send(lows_ref, lows_out.at[me], ls, lr, k, target))
     mine = rows_ref.at[me // per]
@@ -80,7 +108,11 @@
         copy.wait()
 
 
-def gather(n, per, shards, rows, stats, lows):
+def gather(n, per, shards, select, x, g, gain, route, down, up):
+    count, width = x.shape
+    rows = jax.ShapeDtypeStruct(select.shape[:2] + (2 * width,), x.dtype)
+    stats = jax.ShapeDtypeStruct((route.shape[0], count), jnp.float32)
+    lows = jax.ShapeDtypeStruct((count, 2 * down.shape[1]), x.dtype)
     vmem = pl.BlockSpec(memory_space=pltpu.VMEM)
     dma = pltpu.SemaphoreType.DMA
     return pl.pallas_call(
@@ -90,13 +122,13 @@
             jax.ShapeDtypeStruct((n,) + stats.shape, stats.dtype),
             jax.ShapeDtypeStruct((n,) + lows.shape, lows.dtype),
         ),
-        in_specs=[vmem] * 3,
+        in_specs=[vmem] * 7,
         out_specs=(vmem,) * 3,
-        scratch_shapes=[dma((n - 1,))] * 6 + [dma((n,))] * 2 + [dma((3,))],
+        scratch_shapes=[pltpu.VMEM(a.shape, a.dtype) for a in (rows, stats, lows)] + [dma((n - 1,))] * 6 + [dma((n,))] * 2 + [dma((3,))],
         compiler_params=pltpu.CompilerParams(
             collective_id=0, has_side_effects=True, vmem_limit_bytes=VMEM_LIMIT
         ),
-    )(rows, stats, lows)
+    )(select, x, g, gain, route, down, up)
 
 
 def expert_kernel(
@@ -187,9 +219,10 @@
 
 def scatter_kernel(
     n, per, experts, sections,
-    dn_ref, vec_ref, pd_ref, pu_ref, st_ref, tok_ref, base_ref, x_ref, g_ref, gain_ref, rt_ref,
+    dn_ref, vec_ref, select_ref, tok_ref, lows_ref, mask_ref, x_ref, g_ref, gain_ref, rt_ref,
+    down_ref,
     back_out, pd_out, pu_out,
-    pdn, pvec, ppd, ppu, sendbuf, landing, result, ps, pr, qs, qr, es, er, zs, zr,
+    pd_ref, pu_ref, pdn, pvec, ppd, ppu, sendbuf, landing, result, ps, pr, qs, qr, es, er, zs, zr,
 ):
     me = lax.axis_index("expert")
     core = lax.axis_index("dp")
@@ -215,9 +248,6 @@
         send(dn_ref.at[other, peer], pdn.at[k], ps, pr, k, partner)
         for k, peer in enumerate(peers + [me])
     ]
-    shared.append(send(pd_ref, ppd, qs, qr, 1, partner))
-    shared.append(send(pu_ref, ppu, qs, qr, 2, partner))
-
     shared[0].wait()
     v = vec_ref[core] + pvec[...]
     high = v.astype(jnp.bfloat16)
@@ -237,12 +267,32 @@
 
     token = tok_ref[...]
     column = lambda i: token[:, i:i + 1]
+    scale = column(2 * experts + 1)
+    x = x_ref[...].astype(jnp.float32)
+    ranks = down_ref.shape[1]
+    low_all = lows_ref[0].astype(jnp.float32)
+    for j in range(1, n):
+        low_all = low_all + lows_ref[j].astype(jnp.float32)
+    raw_low, g_low = low_all[:, :ranks], low_all[:, ranks:]
+    mask = mask_ref[...]
+    low = (raw_low * scale * mask).astype(jnp.bfloat16)
+    d_low = (ADAPTER_SCALE * g_low * mask).astype(jnp.bfloat16)
+    normed = (x * scale * gain_ref[...]).astype(jnp.bfloat16)
+    pd_ref[...] = lax.dot_general(normed, d_low, FIRST, preferred_element_type=jnp.float32)
+    pu_ref[...] = ADAPTER_SCALE * lax.dot_general(
+        low, g_ref[...], FIRST, preferred_element_type=jnp.float32
+    )
+    shared.append(send(pd_ref, ppd, qs, qr, 1, partner))
+    shared.append(send(pu_ref, ppu, qs, qr, 2, partner))
+    low_stat = jnp.sum(d_low.astype(jnp.float32) * raw_low, axis=1, keepdims=True)
     spread = jnp.zeros_like(column(0))
     stat = jnp.zeros_like(spread)
-    total = base_ref[...]
+    total = lax.dot_general(d_low, down_ref[...], LAST, preferred_element_type=jnp.float32)
 
     def pick(ref_index, values):
-        return jnp.dot(st_ref[ref_index], values, preferred_element_type=jnp.float32)
+        return lax.dot_general(
+            select_ref[ref_index], values, FIRST, preferred_element_type=jnp.float32
+        )
 
     def weights_of(expert):
         gate, sign = jnp.zeros_like(spread), jnp.zeros_like(spread)
@@ -266,12 +316,12 @@
         total, spread, stat = add(
             expert, landing[k, :, :width], landing[k, :, width:], total, spread, stat
         )
-    scale = column(2 * experts + 1)
     delta = spread * column(2 * experts)
     for e in range(experts):
-        total = total + (delta * column(experts + e)) * rt_ref[e:e + 1, :]
-    stat = stat / scale + column(2 * experts + 2) + delta * column(2 * experts + 3)
-    x = x_ref[...].astype(jnp.float32)
+        total = total + (delta * column(experts + e)) * rt_ref[e + 1:e + 2, :].astype(
+            jnp.float32
+        )
+    stat = stat / scale + low_stat + delta * column(2 * experts + 2)
     g = g_ref[...].astype(jnp.float32)
     weighted = total * gain_ref[...]
     out = g + scale * weighted - x * (scale * scale * scale * stat / (n * width))
@@ -284,9 +334,11 @@
     handed.wait()
 
 
-def scatter(n, per, experts, sections, dn, vec, pd, pu, *rest):
+def scatter(n, per, experts, sections, dn, vec, *rest):
     cap, width = dn.shape[2:]
-    x = rest[3]
+    x, down = rest[4], rest[8]
+    pd = jax.ShapeDtypeStruct(down.shape, jnp.float32)
+    pu = jax.ShapeDtypeStruct(down.shape[::-1], jnp.float32)
     vmem = pl.BlockSpec(memory_space=pltpu.VMEM)
     dma = pltpu.SemaphoreType.DMA
     return pl.pallas_call(
@@ -296,9 +348,11 @@
             jax.ShapeDtypeStruct(pd.shape, jnp.float32),
             jax.ShapeDtypeStruct(pu.shape, jnp.float32),
         ),
-        in_specs=[vmem] * (4 + len(rest)),
+        in_specs=[vmem] * (2 + len(rest)),
         out_specs=(vmem,) * 3,
         scratch_shapes=[
+            pltpu.VMEM(pd.shape, jnp.float32),
+            pltpu.VMEM(pu.shape, jnp.float32),
             pltpu.VMEM((n, cap, width), jnp.float32),
             pltpu.VMEM(vec.shape[1:], jnp.float32),
             pltpu.VMEM(pd.shape, jnp.float32),
@@ -312,7 +366,7 @@
         compiler_params=pltpu.CompilerParams(
             collective_id=1, has_side_effects=True, vmem_limit_bytes=VMEM_LIMIT
         ),
-    )(dn, vec, pd, pu, *rest)
+    )(dn, vec, *rest)
 
 
 def body(
@@ -351,30 +405,13 @@
     rank = jnp.dot(before, member.astype(jnp.bfloat16), preferred_element_type=jnp.float32)
     place = jnp.where(member > 0, rank, -1.0)
     slots = jnp.arange(CAP, dtype=jnp.float32)
-    spread_to = (place.T[:, :, None] == slots[None, None, :]).astype(jnp.bfloat16)
     select = (place.T[:, None, :] == slots[None, :, None]).astype(jnp.bfloat16)
 
-    both = jnp.concatenate([x, g], axis=1)
-    rows = jnp.dot(
-        select.reshape(experts * CAP, count), both, preferred_element_type=jnp.float32
-    ).astype(jnp.bfloat16).reshape(experts, CAP, 2 * width)
-    xf = x.astype(jnp.float32)
-    gained = (xf * gain).astype(jnp.bfloat16)
-    square = jnp.sum(xf * xf, axis=1)[None, :]
-    raw = lax.dot_general(
-        route_cols, gained, (((0,), (1,)), ((), ())), preferred_element_type=jnp.float32
-    )
-    fill = -(1 + experts) % 8
-    stats = jnp.concatenate([square, raw, jnp.zeros((fill, count), jnp.float32)], axis=0)
-    lows = jnp.concatenate(
-        [
-            jnp.dot(gained, down, preferred_element_type=jnp.float32),
-            lax.dot_general(g, up_map, LAST, preferred_element_type=jnp.float32),
-        ],
-        axis=1,
-    ).astype(jnp.bfloat16)
-
-    all_rows, all_stats, all_lows = gather(n, per, shards, rows, stats, lows)
+    route_t = jnp.pad(route_cols.T, ((1, -(1 + experts) % 8), (0, 0)))
+
+    all_rows, all_stats, all_lows = gather(
+        n, per, shards, select, x, g, gain, route_t, down, up_map
+    )
 
     dn, vec = expert_back(
         all_rows, layer_norm_gains, expert_gate_weight, expert_up_weight, expert_down_weight
@@ -387,23 +424,14 @@
     raw_spread = jnp.sum(sign * raw_logits, axis=1, keepdims=True)
     upper = jax.nn.sigmoid(raw_spread * scale)
     table = upper * first + (1.0 - upper) * second
-    low_all = jnp.sum(all_lows.astype(jnp.float32), axis=0)
-    raw_low, g_low = low_all[:, :ranks], low_all[:, ranks:]
     mask = job_columns(backward_job_lengths[0], lax.axis_index("dp") * count, count)
-    low = (raw_low * scale * mask).astype(jnp.bfloat16)
-    d_low = (ADAPTER_SCALE * g_low * mask).astype(jnp.bfloat16)
-    normed_cols = (xf * scale * gain).astype(jnp.bfloat16)
-    pu = ADAPTER_SCALE * lax.dot_general(low, g, FIRST, preferred_element_type=jnp.float32)
-    pd = lax.dot_general(normed_cols, d_low, FIRST, preferred_element_type=jnp.float32)
-    base = lax.dot_general(d_low, down, LAST, preferred_element_type=jnp.float32)
-    low_stat = jnp.sum(d_low.astype(jnp.float32) * raw_low, axis=1, keepdims=True)
-    columns = [table, sign, upper * (1.0 - upper), scale, low_stat, raw_spread]
+    columns = [table, sign, upper * (1.0 - upper), scale, raw_spread]
     used = sum(c.shape[1] for c in columns)
     token = jnp.concatenate(columns + [jnp.zeros((count, -used % LANES), jnp.float32)], axis=1)
 
     handed_back, down_grad, up_grad = scatter(
-        n, per, experts, sections, dn, vec, pd, pu,
-        spread_to, token, base, x, g, gain, route_cols.astype(jnp.float32).T,
+        n, per, experts, sections, dn, vec, select, token, all_lows, mask, x, g, gain, route_t,
+        down,
     )
     return (handed_back[None], down_grad[None], up_grad[None])
 

time: 84.9 us -> 75.2 us (0.89)
  matrix products: 8.38 us -> 0.25 us
  other arithmetic: 5.63 us -> 2.15 us
  local copies, waits for them, and re-layouts: 7.86 us -> 10.1 us
    dot_general x7 -> x0, matrix products: 8.13 us -> none  [the longest x1 2.12 us: body(): jnp.dot(select.reshape(experts * CAP, count), both, preferred_element_typ...]
    unnamed x17 -> x10, local copies, waits for them, and re-layouts: 4.9 us -> 6.47 us
    concatenate x2 -> x0, other arithmetic: 1.38 us -> none  [the longest x1 0.71 us: body(): jnp.concatenate([jnp.dot(gained, down, preferred_element_type=jnp.float32...]
    transpose x1 -> x0, other arithmetic: 1.28 us -> none  [body(): route_cols.astype(jnp.float32)]
    reduce_sum x3 -> x0, other arithmetic: 1.23 us -> none  [the longest x1 1.02 us: body(): square = jnp.sum(xf * xf, axis=1)[None, :]]
where the time goes in v2:
time: 75.2 us; the launch traced here: 74.8 us
  Pallas kernels  61.6 us (82%)
  local copies, waits for them, and re-layouts  10.1 us (13%)
  other arithmetic  2.15 us (3%)
    pallas_call x1, Pallas kernels, expert_back(): pl.pallas_call(functools.partial(expert_kernel, n, width), grid=(hidden /...  26.4 us
    pallas_call x1, Pallas kernels, scatter(): pl.pallas_call(functools.partial(scatter_kernel, n, per, experts, section...  18.4 us
    pallas_call x1, Pallas kernels, gather(): pl.pallas_call(functools.partial(gather_kernel, n, per), out_shape=(jax.S...  16.8 us
    unnamed x10, local copies, waits for them, and re-layouts  6.47 us

profile of v2, /device:TPU:0, one launch (start us, length us, event | category | flops | bytes accessed | tf_op | source)
XLA Modules:
  0.0 74.8 jit_solution(5880057725753399901)
XLA Ops:
  0.6 0.0 copy-start
  0.6 0.8 %slice_bitcast_fusion.1 = (s32[128]{0:T(128)S(1)}, s32[128]{0:T(128)S(1)}) fusion(s32[128,2]{0,1:T(2,128)} %bitcast.33), kind=kLoop, calls=%fused_computation.33 | loop fusion | bytes 2048 | tf_op jit(solution)/shard_map/eq | solution.py:400
  1.4 0.2 convolution_select_fusion
  1.7 0.7 fusion.select_ref
  2.3 1.3 %constant_dynamic-slice_fusion.gain_ref = f32[1,512]{1,0:T(1,128)} fusion(f32[1,2048]{1,0:T(1,128)} %gain_ref.1, s32[]{:T(128)S(6)} %select_n.19), kind=kLoop, calls=%fused_computation.31 | loop fusion | bytes 4100 | tf_op jit(solution)/shard_map/dynamic_slice | solution.py:394
  3.6 0.0 copy-done
  3.6 0.6 pad.4.route_ref.rt_ref
  4.2 1.6 %copy.32 = bf16[1,512,64]{2,1,0:T(8,128)(2,1)} copy(bf16[1,512,64]{1,2,0:T(8,128)(2,1)} %param.20) | data formatting | bytes 131072 | tf_op args[9]
  5.8 16.8 %shard_map.130 = (bf16[2,4,80,1024]{3,2,1,0:T(8,128)(2,1)}, f32[4,8,128]{2,1,0:T(8,128)}, bf16[4,128,128]{2,1,0:T(8,128)(2,1)}) custom-call(bf16[4,80,128]{2,1,0:T(8,128)(2,1)} %fusion.select_ref, bf16[128,512]{1,0:T(8,128)(2,1)} %bitcast.24, bf16[128,512]{1,0:T(8,128)(2,1)} %bitcast.26, f32[1,512]{1,0:T(1,128)} %constant_dynamic-slice_fusion.gain_ref, ...), custom_call_target="tpu_custom_call" | custom-call | tf_op jit(solution)/shard_map/pallas_call | solution.py:118
  22.6 0.0 copy-start.1
  22.6 0.0 copy-start.2
  22.6 26.4 %shard_map.131 = (f32[2,4,80,512]{3,2,1,0:T(8,128)}, f32[2,80,128]{2,1,0:T(8,128)}) custom-call(bf16[2,4,80,1024]{3,2,1,0:T(8,128)(2,1)} %get-tuple-element.11.rows_ref, f32[1,2048]{1,0:T(1,128)} %gain_ref.1, bf16[1,2048,3584]{2,1,0:T(8,128)(2,1)} %wg_ref.1, bf16[1,2048,3584]{2,1,0:T(8,128)(2,1)} %wu_ref.1, bf16[1,3584,2048]{2,1,0:T(8,128)(2,1)} %wd_ref.1), custom_call_target="tpu_custom_call" | custom-call | tf_op jit(solution)/shard_map/pallas_call | solution.py:190
  49.1 0.0 copy-done.1
  49.1 0.1 copy.33
  49.2 0.2 fusion.4
  49.4 0.1 copy.34
  49.6 0.1 fusion.8
  49.7 0.1 convert_subtract_fusion
  49.9 0.8 %concatenate.3.tok_ref = f32[128,128]{1,0:T(8,128)} concatenate(f32[128,4]{1,0:T(8,128)S(1)} %get-tuple-element.40, f32[128,4]{1,0:T(8,128)S(1)} %get-tuple-element.39, f32[128,1]{1,0:T(8,128)S(1)} %get-tuple-element.36, f32[128,1]{1,0:T(8,128)S(1)} %get-tuple-element.38, f32[128,1]{1,0:T(8,128)S(1)} %copy.34, f32[128,117]{1,0:T(8,128)S(1)} %broadcast_in_dim.16), dimensions={1} | concatenate | bytes 131072 | tf_op jit(solution)/shard_map/concatenate | solution.py:430
  50.6 0.0 copy-done.2
  50.6 0.2 reduce-window.8
  50.8 0.1 convert_reduce_fusion
  50.9 0.7 compare_convert_fusion.mask_ref
  51.6 18.4 %shard_map.132 = (bf16[128,512]{1,0:T(8,128)(2,1)}, f32[512,64]{1,0:T(8,128)}, f32[64,512]{1,0:T(8,128)}) custom-call(f32[2,4,80,512]{3,2,1,0:T(8,128)} %get-tuple-element.12.dn_ref, f32[2,80,128]{2,1,0:T(8,128)} %get-tuple-element.13.vec_ref, bf16[4,80,128]{2,1,0:T(8,128)(2,1)} %fusion.select_ref, f32[128,128]{1,0:T(8,128)} %concatenate.3.tok_ref, ...), custom_call_target="tpu_custom_call" | custom-call | tf_op jit(solution)/shard_map/pallas_call | solution.py:344
  70.0 1.7 %copy.39 = f32[1,512,64]{1,2,0:T(8,128)} copy(f32[1,512,64]{2,1,0:T(8,128)} %bitcast.28) | data formatting | bytes 262144
  71.7 1.6 %copy.42 = bf16[1,128,512]{2,1,0:T(8,128)(2,1)} copy(bf16[1,128,512]{2,1,0:T(8,128)(2,1)} %bitcast.30) | data formatting | bytes 262144
  73.3 1.6 %copy.43 = f32[1,64,512]{2,1,0:T(8,128)} copy(f32[1,64,512]{2,1,0:T(8,128)} %bitcast.29) | data formatting | bytes 262144
  (6 shorter events, 0.1 us)
Async XLA Ops:
  0.6 3.0 %copy-start = (bf16[1,2048,4]{1,2,0:T(4,128)(2,1)S(1)}, bf16[1,2048,4]{1,2,0:T(4,128)(2,1)}, u32[]{:S(2)}) copy-start(bf16[1,2048,4]{1,2,0:T(4,128)(2,1)} %param.16) | copy-start | bytes 49156
  22.6 26.5 %copy-start.1 = (f32[4,8,128]{2,1,0:T(8,128)S(1)}, f32[4,8,128]{2,1,0:T(8,128)}, u32[]{:S(2)}) copy-start(f32[4,8,128]{2,1,0:T(8,128)} %get-tuple-element.14) | copy-start | bytes 49156
  22.6 28.0 %copy-start.2 = (s32[1,4]{1,0:T(1,128)S(1)}, s32[1,4]{1,0:T(1,128)}, u32[]{:S(2)}) copy-start(s32[1,4]{1,0:T(1,128)} %param.14) | copy-start | bytes 52
